TPU v7x, 32 devices: a whole 2x2x4 slice. The times are simulated.
32 devices in a mesh: grp: 2 (over y), seq: 4 (over z), head: 2 (over x), rep: 2 (over core).
Axes of the slice: x: 2, y: 2, z: 4, core: 2. Of those that a mesh axis runs over, the one named last changes fastest.
Arguments:
- x_proj: bfloat16 [4, 4, 4, 32, 8192], P(('grp', 'rep'), None, 'seq', None, 'head'), parts along dimension 0, may hold values from -6 to 6
- gate_proj: bfloat16 [4, 4, 4, 32, 8192], P(('grp', 'rep'), None, 'seq', None, 'head'), parts along dimension 0, may hold values from -6 to 6
- bc_proj: bfloat16 [4, 4, 4, 32, 256], P(('grp', 'rep'), None, 'seq'), parts along dimension 0, may hold values from -6 to 6
- dt_proj: bfloat16 [4, 4, 4, 32, 128], P(('grp', 'rep'), None, 'seq', None, 'head'), parts along dimension 0, may hold values from -5.5 to 7.5
- a_rate: float32 [128], P('head'), may hold values from 0.0001953125 to 0.05
- dt_bias: float32 [128], P('head'), may hold values from -1 to 1
- d_skip: float32 [128], P('head'), may hold values from 0.5 to 1.5
- conv_x_weight: float32 [4, 8192], P(None, 'head'), may hold values from -3 to 3
- conv_bc_weight: float32 [4, 256], replicated, may hold values from -3 to 3
- norm_gain: float32 [8192], P('head'), may hold values from 0.1 to 1.9
- out_weight: bfloat16 [8192, 2048], P(('seq', 'rep'), 'head'), may hold values from -0.0625 to 0.0625
- request_first_position: int32 [4], P(('grp', 'rep')), parts along dimension 0, may hold values from 0 to 255
- owner: int32 [4, 4], P(('grp', 'rep')), parts along dimension 0, may hold values from 0 to 3, each once within a row
Outputs:
- mixed: bfloat16 [4, 512, 2048], P(('grp', 'rep'), 'seq', 'head'), parts along dimension 0
- ssm_state: float32 [4, 4, 128, 2048], P(('grp', 'rep'), 'seq', 'head'), parts along dimension 0
- conv_x_state: bfloat16 [4, 4, 3, 2048], P(('grp', 'rep'), 'seq', None, 'head'), parts along dimension 0
- conv_bc_state: bfloat16 [4, 4, 3, 64], P(('grp', 'rep'), 'seq'), parts along dimension 0
There are 2 independent parts, one for each index of `grp`. A program takes and returns all parts, laid end to end along the dimension named above; an argument that names none is the same for every part. Nothing has to cross between parts.
Inputs may be any that keep to these rules, and one draw needn't show every extreme that they name: Each row of owner names every index of seq once.
All inputs are finite; a program needn't handle non-finite values.
Results may differ from a plain program's by a relative error of at most 0.007.
Values may be sent and summed in bfloat16 or wider, within the bound.
No kernel may reach another device: no remote copies, remote signals or barrier semaphores. Data moves between devices by JAX's collectives and lax.ppermute only.
A program may use at most 128 MiB of HBM per device.

v0:
```python
import jax
import jax.numpy as jnp
from jax import lax
from jax.sharding import PartitionSpec as P

HEAD_DIM = 64
NSTATE = 128
KCONV = 4
SPAN = 128
INNER = 8192


highest = lax.Precision.HIGHEST
stability_constant = 1e-05


def passed_along(value, axis, by):
    devices = lax.axis_size(axis)
    pairs = [(i, i + by) for i in range(devices) if 0 <= i + by < devices]
    return lax.ppermute(value, axis, pairs)


def prefix(value, axis, combine, identity, reverse):
    devices, place = (lax.axis_size(axis), lax.axis_index(axis))
    everything = jax.tree.map(lambda part: lax.all_gather(part, axis), value)
    start = jax.tree.map(
        lambda part, zero: jnp.broadcast_to(jnp.asarray(zero, part.dtype), part.shape),
        value,
        identity,
    )

    def lap(k, before):
        at = devices - 1 - k if reverse else k
        reached = at > place if reverse else at < place
        new = combine(before, jax.tree.map(lambda part: part[at], everything))
        return jax.tree.map(lambda a, b: jnp.where(reached, a, b), new, before)

    return lax.fori_loop(0, devices, lap, start)


def broadcast(block, axis, source):
    block = jnp.where(lax.axis_index(axis) == source, block, jnp.zeros_like(block))
    return lax.psum(block, axis)


def span_terms(x_conv, b_rows, c_rows, step_size, log_decay):
    cum_decay = jnp.cumsum(log_decay, axis=1)
    scores = jnp.einsum("kqn,ktn->kqt", c_rows, b_rows, preferred_element_type=jnp.float32)
    cum_heads = jnp.swapaxes(cum_decay, 1, 2)
    step_heads = jnp.swapaxes(step_size, 1, 2)
    block_len = cum_decay.shape[1]
    causal = jnp.arange(block_len)[:, None] >= jnp.arange(block_len)[None, :]
    decay_gap = cum_heads[:, :, :, None] - cum_heads[:, :, None, :]
    seg_decay = jnp.exp(jnp.where(causal, decay_gap, -jnp.inf))
    weights = (scores[:, None] * seg_decay * step_heads[:, :, None, :]).astype(jnp.bfloat16)
    y_intra = jnp.einsum("khqt,kthp->kqhp", weights, x_conv, preferred_element_type=jnp.float32)
    remaining_length = jnp.exp(cum_decay[:, -1:, :] - cum_decay)
    scaled = ((remaining_length * step_size)[..., None] * x_conv.astype(jnp.float32)).astype(
        jnp.bfloat16
    )
    states = jnp.einsum("kthp,ktn->khpn", scaled, b_rows, preferred_element_type=jnp.float32)
    return (cum_decay, y_intra, states, jnp.exp(cum_decay[:, -1, :]))


def conv_silu(preceding_tokens, current, weight):
    extended = jnp.concatenate([preceding_tokens, current], axis=0)
    length = current.shape[0]
    accum = jnp.zeros(current.shape, jnp.float32)
    for offset in range(weight.shape[0]):
        accum = accum + weight[offset] * extended[offset : offset + length].astype(jnp.float32)
    return jax.nn.silu(accum)


def link(preceding_tokens, later):
    return (
        preceding_tokens[0] * later[0],
        later[0][:, None, None] * preceding_tokens[1] + later[1],
    )


def multiply(preceding_tokens, later):
    return preceding_tokens * later


def add_rows(source, piece):
    return jnp.dot(source, piece, preferred_element_type=jnp.float32)


def take_slab(values, slab_index, seq_count):
    grouped = values.reshape(values.shape[0], seq_count, -1)
    return lax.dynamic_index_in_dim(grouped, slab_index, axis=1, keepdims=False)


def local(
    x_proj,
    gate_proj,
    bc_proj,
    dt_proj,
    a_rate,
    dt_bias,
    d_skip,
    conv_x_weight,
    conv_bc_weight,
    norm_gain,
    out_weight,
    request_first_position,
    owner,
):
    x_all, z_all, bc_all, dt_all = (
        lax.all_to_all(x_proj, "seq", split_axis=1, concat_axis=2, tiled=True),
        lax.all_to_all(gate_proj, "seq", split_axis=1, concat_axis=2, tiled=True),
        lax.all_to_all(bc_proj, "seq", split_axis=1, concat_axis=2, tiled=True),
        lax.all_to_all(dt_proj, "seq", split_axis=1, concat_axis=2, tiled=True),
    )
    tokens_here = x_all.shape[2] * x_all.shape[3]
    x_local = x_all.reshape(tokens_here, x_all.shape[4])
    z_local = z_all.reshape(tokens_here, z_all.shape[4])
    bc_local = bc_all.reshape(tokens_here, bc_all.shape[4])
    dt_local = dt_all.reshape(tokens_here, dt_all.shape[4])
    heads = dt_local.shape[1]
    seq_index = lax.axis_index("seq")
    seq_count = lax.axis_size("seq")
    positions = seq_index * tokens_here + jnp.arange(tokens_here, dtype=jnp.int32)
    is_live = positions >= request_first_position[0]
    x_live = jnp.where(is_live[:, None], x_local, jnp.zeros_like(x_local))
    bc_live = jnp.where(is_live[:, None], bc_local, jnp.zeros_like(bc_local))
    rim_rows = KCONV - 1
    tail_x = x_live[tokens_here - rim_rows :]
    tail_bc = bc_live[tokens_here - rim_rows :]
    before_x, before_bc = passed_along((tail_x, tail_bc), "seq", 1)
    x_conv = conv_silu(before_x, x_live, conv_x_weight).astype(jnp.bfloat16)
    bc_conv = conv_silu(before_bc, bc_live, conv_bc_weight).astype(jnp.bfloat16)
    step_size = (
        jax.nn.softplus(dt_local.astype(jnp.float32) + dt_bias)
        * is_live.astype(jnp.float32)[:, None]
    )
    log_decay = -a_rate * step_size
    blocks = tokens_here // SPAN
    x_blocks = x_conv.reshape(blocks, SPAN, heads, HEAD_DIM)
    b_blocks = bc_conv[:, :NSTATE].reshape(blocks, SPAN, NSTATE)
    c_blocks = bc_conv[:, NSTATE:].reshape(blocks, SPAN, NSTATE)
    cum_decay, y_intra, states, decays = span_terms(
        x_blocks,
        b_blocks,
        c_blocks,
        step_size.reshape(blocks, SPAN, heads),
        log_decay.reshape(blocks, SPAN, heads),
    )

    def advance(carry, inputs):
        factor, contrib = inputs
        return (factor[:, None, None] * carry + contrib, carry)

    zero_state = jnp.zeros((heads, HEAD_DIM, NSTATE), jnp.float32)
    local_final, local_enter = lax.scan(advance, zero_state, (decays, states))
    dev_decay = jnp.prod(decays, axis=0)
    ones_heads = jnp.ones((heads,), jnp.float32)
    enter_decay, enter_state = prefix(
        (dev_decay, local_final), "seq", link, (ones_heads, zero_state), False
    )
    c_wide = c_blocks.astype(jnp.float32)
    before_block = jnp.concatenate([ones_heads[None], jnp.cumprod(decays, axis=0)[:-1]], axis=0)
    entering = local_enter + before_block[:, :, None, None] * enter_state[None]
    y_state = jnp.exp(cum_decay)[..., None] * jnp.einsum(
        "kqn,khpn->kqhp", c_wide, entering, precision=highest
    )
    y_total = y_intra + y_state + d_skip[:, None] * x_blocks.astype(jnp.float32)
    y_flat = y_total.reshape(tokens_here, heads * HEAD_DIM)
    gated = y_flat * jax.nn.silu(z_local.astype(jnp.float32))
    square_sums = lax.psum(jnp.sum(gated * gated, axis=1), "head")
    normed = (
        gated * lax.rsqrt(square_sums[:, None] / INNER + stability_constant) * norm_gain
    ).astype(jnp.bfloat16)
    last_index = seq_count - 1
    after_decay = prefix(dev_decay, "seq", multiply, ones_heads, True)
    final_state = lax.psum(after_decay[:, None, None] * local_final, "seq")
    keep_x, keep_bc = (broadcast(tail_x, "seq", last_index), broadcast(tail_bc, "seq", last_index))
    slab_index = jnp.sum(
        jnp.where(owner[0] == seq_index, jnp.arange(seq_count, dtype=jnp.int32), 0)
    )
    ssm_state = take_slab(final_state.reshape(heads, -1), slab_index, seq_count)[None, None]
    conv_x_state = take_slab(keep_x, slab_index, seq_count)[None, None]
    conv_bc_state = take_slab(keep_bc, slab_index, seq_count)[None, None]
    features = lax.all_gather(normed, "head", axis=1, tiled=True)
    out_cols = out_weight.shape[1]
    mixed_sum = add_rows(features, lax.all_gather(out_weight, ("seq", "rep"), axis=0, tiled=True))
    mixed = mixed_sum.astype(jnp.bfloat16).reshape(1, tokens_here, out_cols)
    return (mixed, ssm_state, conv_x_state, conv_bc_state)


def solution(mesh):
    return jax.shard_map(
        local,
        mesh=mesh,
        in_specs=(
            P(("grp", "rep"), None, "seq", None, "head"),
            P(("grp", "rep"), None, "seq", None, "head"),
            P(("grp", "rep"), None, "seq", None, None),
            P(("grp", "rep"), None, "seq", None, "head"),
            P("head"),
            P("head"),
            P("head"),
            P(None, "head"),
            P(),
            P("head"),
            P(("seq", "rep"), "head"),
            P(("grp", "rep")),
            P(("grp", "rep"), None),
        ),
        out_specs=(
            P(("grp", "rep"), "seq", "head"),
            P(("grp", "rep"), "seq", "head", None),
            P(("grp", "rep"), "seq", None, "head"),
            P(("grp", "rep"), "seq", None, None),
        ),
        check_vma=False,
    )
```

profile of v0, /device:TPU:0, one launch (start us, length us, event | category | flops | bytes accessed | tf_op | source)
XLA Modules:
  0.0 532.8 jit_solution(8478039113186121479)
XLA Ops:
  7.2 0.7 copy-done
  7.9 0.7 reshape.454
  8.6 6.3 %all-to-all-start.2 = ((bf16[4,2,1024]{2,1,0:T(2,128)(2,1)}), bf16[4,2,1024]{2,1,0:T(2,128)(2,1)S(1)}, u32[]{:S(2)}, u32[]{:S(2)}) async-start(bf16[4,2,1024]{2,1,0:T(2,128)(2,1)} %reshape.454), calls=%async_computation.2 | async-start | bytes 32768 | tf_op jit(solution)/shard_map/all_to_all | solution.py:113
  15.6 1.7 fusion.36
  17.3 1.4 fusion.37
  20.6 4.5 all-to-all-start.1
  25.2 0.7 broadcast_multiply_fusion.1
  26.1 0.7 bitcast_exponential_fusion
  27.1 1.9 copy.80
  29.0 11.5 %all-gather = f32[4,1,64]{2,1,0:T(1,128)S(1)} all-gather(f32[1,1,64]{2,1,0:T(1,128)S(1)} %get-tuple-element.290), channel_id=2, replica_groups=mesh['grp'=2,'seq'=4,'head'=2,'rep'=2] {'seq'}, dimensions={0}, use_global_device_ids=true | all-gather | bytes 1280 | tf_op jit(solution)/shard_map/all_gather | solution.py:25
  40.5 3.7 all-to-all-start
  45.0 0.9 bitcast_select_fusion.1
  46.6 3.8 collective-permute-start.1
  50.4 16.6 %all-to-all-done = bf16[1,4,1,32,4096]{4,3,2,0,1:T(8,128)(2,1)S(1)} async-done(((bf16[1,4,1,32,4096]{4,3,2,0,1:T(8,128)(2,1)}), bf16[1,4,1,32,4096]{4,3,2,0,1:T(8,128)(2,1)S(1)}, u32[]{:S(2)}, u32[]{:S(2)}) %all-to-all-start) | async-done | bytes 1048608 | tf_op jit(solution)/shard_map/all_to_all | solution.py:110
  67.3 1.3 collective-permute-start
  69.2 0.9 multiply_convert_fusion.4
  70.2 3.1 multiply_convert_fusion.2
  73.3 1.6 copy.81
  74.9 2.4 broadcast_multiply_fusion
  77.3 5.7 %all-to-all-start.3 = ((bf16[1,4,1,32,4096]{4,3,2,0,1:T(8,128)(2,1)}), bf16[1,4,1,32,4096]{4,3,2,0,1:T(8,128)(2,1)}, u32[]{:S(2)}, u32[]{:S(2)}) async-start(bf16[1,4,1,32,4096]{4,3,2,0,1:T(8,128)(2,1)} %bitcast.35), calls=%async_computation.3 | async-start | bytes 2097152 | tf_op jit(solution)/shard_map/all_to_all | solution.py:111
  83.5 48.3 %all-to-all-done.3 = bf16[1,4,1,32,4096]{4,3,2,0,1:T(8,128)(2,1)} async-done(((bf16[1,4,1,32,4096]{4,3,2,0,1:T(8,128)(2,1)}), bf16[1,4,1,32,4096]{4,3,2,0,1:T(8,128)(2,1)}, u32[]{:S(2)}, u32[]{:S(2)}) %all-to-all-start.3) | async-done | bytes 1048608 | tf_op jit(solution)/shard_map/all_to_all | solution.py:111
  131.8 2.7 bitcast_convert_fusion
  134.6 4.6 reshape.449
  139.2 4.8 copy.87
  144.0 1.3 copy.72
  145.3 1.7 copy.82
  147.0 3.0 reshape_reshape.3
  150.0 1.1 copy-done.4
  151.2 3.3 fusion.1
  154.4 87.4 %all-gather.10.cloned.1.call-done = f32[256,64,128]{2,1,0:T(8,128)} async-done(((f32[64,64,128]{2,1,0:T(8,128)}), f32[256,64,128]{2,1,0:T(8,128)}) %all-gather.10.cloned.1.call-update) | async-done | bytes 8388624 | tf_op jit(solution)/shard_map/all_gather | solution.py:25
  241.9 11.4 %while.35 = (s32[]{:T(128)}, f32[64,64,128]{2,1,0:T(8,128)S(1)}, s32[]{:T(128)}, f32[4,64]{1,0:T(4,128)}, f32[4,64,64,128]{3,2,1,0:T(8,128)}, /*index=5*/s32[]{:T(128)}, s32[]{:T(128)}) while((s32[]{:T(128)}, f32[64,64,128]{2,1,0:T(8,128)S(1)}, s32[]{:T(128)}, f32[4,64]{1,0:T(4,128)}, f32[4,64,64,128]{3,2,1,0:T(8,128)}, ...), condition=%wide.region_2.3_spmd.clone, body=%wide.region_1.2_spmd.clone.sunk | while | flops 2097156 | bytes 6292329 | solution.py:38
  241.9 0.7 dynamic-slice_bitcast_fusion.4
  242.6 2.1 fusion.44
  244.7 0.7 dynamic-slice_bitcast_fusion.4
  245.3 2.1 fusion.44
  248.1 2.3 fusion.44
  251.1 2.1 fusion.44
  253.2 5.9 %multiply_reduce_fusion = (f32[128]{0:T(128)S(1)}, f32[1,128,64,64]{1,3,2,0:T(8,128)}) fusion(f32[1,128,64,64]{1,3,2,0:T(8,128)} %copy.87, f32[1,128,64,64]{1,3,2,0:T(8,128)} %bitcast.133, f32[64]{0:T(128)S(1)} %copy-done.18, f32[64,64,128]{2,1,0:T(8,128)S(1)} %get-tuple-element.223, bf16[128,256]{1,0:T(8,128)(2,1)S(1)} %multiply_convert_fusion.4, ...), kind=kOutput, calls=%fused_computation.17 | convolution fusion | flops 811073408 | bytes 10552320 | tf_op jit(solution)/shard_map/kqn,khpn->kqhp/dot_general | solution.py:164
  259.1 3.1 copy.85
  262.2 4.9 psum.28
  267.1 3.3 fusion.14
  273.7 18.3 %all-reduce = (bf16[3,4,1024]{2,0,1:T(4,128)(2,1)S(1)}, bf16[3,4,64]{2,0,1:T(4,128)(2,1)S(1)}) all-reduce(bf16[3,4,1024]{2,0,1:T(4,128)(2,1)S(1)} %bitcast.140, bf16[3,4,64]{2,0,1:T(4,128)(2,1)S(1)} %copy.89), channel_id=1, replica_groups=mesh['grp'=2,'seq'=4,'head'=2,'rep'=2] {'seq'}, use_global_device_ids=true, to_apply=%region_9.10 | all-reduce | flops 13056 | bytes 52224 | tf_op jit(solution)/shard_map/psum | solution.py:43
  293.2 37.3 %all-reduce.3.cloned.1.call-done = f32[64,4,2048]{2,1,0:T(4,128)} async-done(((f32[64,4,2048]{2,1,0:T(4,128)}), f32[64,4,2048]{2,1,0:T(4,128)}) %all-reduce.3.cloned.1.call-update) | async-done | bytes 2097168 | tf_op jit(solution)/shard_map/psum | solution.py:176
  330.5 2.1 constant_dynamic-slice_fusion
  332.7 1.0 copy.92
  333.6 30.6 %all-gather.6.cloned.1.call-done = bf16[128,8192]{1,0:T(8,128)(2,1)} async-done(((bf16[128,4096]{1,0:T(8,128)(2,1)}), bf16[128,8192]{1,0:T(8,128)(2,1)}) %all-gather.6.cloned.1.call-update) | async-done | bytes 2097168 | tf_op jit(solution)/shard_map/all_gather | solution.py:184
  364.2 152.6 %all-gather.8.cloned.1.call-done = bf16[8192,1024]{1,0:T(8,128)(2,1)} async-done(((bf16[1024,1024]{1,0:T(8,128)(2,1)}), bf16[8192,1024]{1,0:T(8,128)(2,1)}) %all-gather.8.cloned.1.call-update) | async-done | bytes 16777232 | tf_op jit(solution)/shard_map/all_gather | solution.py:186
  516.8 9.5 %fusion.16 = bf16[1,128,1024]{2,1,0:T(8,128)(2,1)} fusion(bf16[128,8192]{1,0:T(8,128)(2,1)} %all-gather.6.cloned.1.call-done, bf16[8192,1024]{1,0:T(8,128)(2,1)} %all-gather.8.cloned.1.call-done), kind=kOutput, calls=%fused_computation.31 | convolution fusion | flops 2147614720 | bytes 19136512 | tf_op jit(solution)/shard_map/dot_general | solution.py:86
  (83 shorter events, 9.2 us)
Async XLA Ops:
  7.2 0.8 copy-start
  8.6 12.0 %all-to-all-start.2 = ((bf16[4,2,1024]{2,1,0:T(2,128)(2,1)}), bf16[4,2,1024]{2,1,0:T(2,128)(2,1)S(1)}, u32[]{:S(2)}, u32[]{:S(2)}) async-start(bf16[4,2,1024]{2,1,0:T(2,128)(2,1)} %reshape.454), calls=%async_computation.2 | async-start | bytes 32768 | tf_op jit(solution)/shard_map/all_to_all | solution.py:113
  19.3 7.5 %copy-start.11 = (f32[128]{0:T(128)}, f32[128]{0:T(128)S(1)}, u32[]{:S(2)}) copy-start(f32[128]{0:T(128)S(1)} %get-tuple-element.282) | copy-start | bytes 1540
  20.6 19.9 %all-to-all-start.1 = ((bf16[1,4,1,32,256]{4,3,2,0,1:T(8,128)(2,1)}), bf16[1,4,1,32,256]{4,3,2,0,1:T(8,128)(2,1)S(1)}, u32[]{:S(2)}, u32[]{:S(2)}) async-start(bf16[1,4,1,32,256]{4,3,2,0,1:T(8,128)(2,1)} %bitcast.145), calls=%async_computation.1 | async-start | bytes 131072 | tf_op jit(solution)/shard_map/all_to_all | solution.py:112
  29.0 15.8 %copy-start.6 = (f32[64]{0:T(128)S(1)}, f32[64]{0:T(128)}, u32[]{:S(2)}) copy-start(f32[64]{0:T(128)} %custom-call.1) | copy-start | bytes 772
  29.0 16.0 %copy-start.15 = (pred[128]{0:T(512)(128)(4,1)S(1)}, pred[128]{0:T(512)(128)(4,1)}, u32[]{:S(2)}) copy-start(pred[128]{0:T(512)(128)(4,1)} %get-tuple-element.283) | copy-start | bytes 388
  40.5 4.5 copy-start.5
  40.5 29.6 %copy-start.3 = (f32[128,4096]{1,0:T(8,128)S(1)}, f32[128,4096]{1,0:T(8,128)}, u32[]{:S(2)}) copy-start(f32[128,4096]{1,0:T(8,128)} %copy.80) | copy-start | bytes 6291460
  40.5 26.5 %all-to-all-start = ((bf16[1,4,1,32,4096]{4,3,2,0,1:T(8,128)(2,1)}), bf16[1,4,1,32,4096]{4,3,2,0,1:T(8,128)(2,1)S(1)}, u32[]{:S(2)}, u32[]{:S(2)}) async-start(bf16[1,4,1,32,4096]{4,3,2,0,1:T(8,128)(2,1)} %bitcast.135), calls=%async_computation | async-start | bytes 2097152 | tf_op jit(solution)/shard_map/all_to_all | solution.py:110
  44.2 197.7 %all-gather.10.cloned.1.call-start = ((), (), s32[]{:S(2)}) async-start(), calls=%async_computation.7 | async-start | bytes 10485760 | tf_op jit(solution)/shard_map/all_gather | solution.py:25
  45.0 22.0 %copy-start.7 = (f32[64]{0:T(128)}, f32[64]{0:T(128)S(1)}, u32[]{:S(2)}) copy-start(f32[64]{0:T(128)S(1)} %get-tuple-element.224) | copy-start | bytes 772
  45.0 22.0 %copy-start.10 = (f32[4,64]{1,0:T(4,128)}, f32[4,64]{1,0:T(4,128)S(1)}, u32[]{:S(2)}) copy-start(f32[4,64]{1,0:T(4,128)S(1)} %get-tuple-element.430) | copy-start | bytes 3076
  46.6 22.0 %collective-permute-start.1 = (bf16[3,256]{1,0:T(4,128)(2,1)S(1)}, bf16[3,256]{1,0:T(4,128)(2,1)S(1)}, u32[]{:S(2)}, u32[]{:S(2)}) collective-permute-start(bf16[3,256]{1,0:T(4,128)(2,1)S(1)} %get-tuple-element.287), channel_id=1, source_target_pairs={{0,4},{4,8},{8,12},{1,5},{5,9},{9,13},{2,6},{6,10},{10,14},{3,7},{... | collective-permute-start | bytes 4616 | tf_op jit(solution)/shard_map/ppermute | solution.py:20
  67.3 2.9 collective-permute-start
  68.6 0.6 copy-start.16
  73.3 1.6 copy-start.8
  73.3 1.6 copy-start.17
  77.3 5.7 %copy-start.12 = (f32[128]{0:T(128)S(1)}, f32[128]{0:T(128)}, u32[]{:S(2)}) copy-start(f32[128]{0:T(128)} %copy-done.11) | copy-start | bytes 1540
  77.3 5.8 %copy-start.14 = (f32[64]{0:T(128)S(1)}, f32[64]{0:T(128)}, u32[]{:S(2)}) copy-start(f32[64]{0:T(128)} %param.22) | copy-start | bytes 772
  77.3 54.5 %all-to-all-start.3 = ((bf16[1,4,1,32,4096]{4,3,2,0,1:T(8,128)(2,1)}), bf16[1,4,1,32,4096]{4,3,2,0,1:T(8,128)(2,1)}, u32[]{:S(2)}, u32[]{:S(2)}) async-start(bf16[1,4,1,32,4096]{4,3,2,0,1:T(8,128)(2,1)} %bitcast.35), calls=%async_computation.3 | async-start | bytes 2097152 | tf_op jit(solution)/shard_map/all_to_all | solution.py:111
  83.0 247.5 %all-reduce.3.cloned.1.call-start = ((), (), s32[]{:S(2)}) async-start(), calls=%async_computation.6 | async-start | bytes 4194304 | tf_op jit(solution)/shard_map/psum | solution.py:176
  149.9 1.2 copy-start.4
  150.0 214.3 %all-gather.6.cloned.1.call-start = ((), (), s32[]{:S(2)}) async-start(), calls=%async_computation.4 | async-start | bytes 3145728 | tf_op jit(solution)/shard_map/all_gather | solution.py:184
  241.9 11.4 %copy-start.18 = (f32[64]{0:T(128)S(1)}, f32[64]{0:T(128)}, u32[]{:S(2)}) copy-start(f32[64]{0:T(128)} %param.23) | copy-start | bytes 772
  259.1 8.0 %copy-start.2 = (f32[1,4,1,32,4096]{4,3,1,2,0:T(8,128)S(1)}, f32[1,4,1,32,4096]{4,3,1,2,0:T(8,128)}, u32[]{:S(2)}) copy-start(f32[1,4,1,32,4096]{4,3,1,2,0:T(8,128)} %bitcast_convert_fusion) | copy-start | bytes 6291460
  259.1 8.0 %copy-start.9 = (f32[4096]{0:T(1024)S(1)}, f32[4096]{0:T(1024)}, u32[]{:S(2)}) copy-start(f32[4096]{0:T(1024)} %param.26) | copy-start | bytes 49156
  270.4 0.7 copy-start.19
  270.4 3.2 copy-start.13
  270.4 246.4 %all-gather.8.cloned.1.call-start = ((), (), s32[]{:S(2)}) async-start(), calls=%async_computation.5 | async-start | bytes 18874368 | tf_op jit(solution)/shard_map/all_gather | solution.py:186
  516.8 9.5 %copy-start.1 = (bf16[1,4,1,32,64]{4,3,2,1,0:T(8,128)(2,1)S(1)}, bf16[1,4,1,32,64]{4,3,2,1,0:T(8,128)(2,1)}, u32[]{:S(2)}) copy-start(bf16[1,4,1,32,64]{4,3,2,1,0:T(8,128)(2,1)} %param.20) | copy-start | bytes 49156
Sparse Core Ops, SparseCore 0:
  77.4 164.3 all-gather.9
  244.2 86.2 all-reduce.2
  332.1 32.1 all-gather.5
  365.7 151.0 all-gather.7
where the time goes:
time: 534 us; the launch traced here: 533 us
  waiting for transfers between devices  374 us (70%)
  local copies, waits for them, and re-layouts  36.1 us (7%)
  blocking collectives  34.7 us (6%)
  starting transfers between devices  25.4 us (5%)
  other arithmetic  24.6 us (5%)
  matrix products  21.1 us (4%)
  between operations  16.6 us (3%)
    all_gather x1, waiting for transfers between devices, local(): lax.all_gather(out_weight, ('seq', 'rep'), axis=0, tiled=True)  153 us
    all_gather x1, waiting for transfers between devices, prefix(): everything = jax.tree.map(lambda part: lax.all_gather(part, axis), value)  87.4 us
    all_to_all x1, waiting for transfers between devices, local(): lax.all_to_all(gate_proj, 'seq', split_axis=1, concat_axis=2, tiled=True)  48.3 us
    psum x1, waiting for transfers between devices, local(): final_state = lax.psum(after_decay[:, None, None] * local_final, 'seq')  37.3 us
    all_gather x1, waiting for transfers between devices, local(): features = lax.all_gather(normed, 'head', axis=1, tiled=True)  30.6 us
    psum x1, blocking collectives, broadcast(): return lax.psum(block, axis)  18.3 us
    all_to_all x1, waiting for transfers between devices, local(): lax.all_to_all(x_proj, 'seq', split_axis=1, concat_axis=2, tiled=True)  16.6 us
    all_gather x1, blocking collectives, prefix(): everything = jax.tree.map(lambda part: lax.all_gather(part, axis), value)  11.5 us
  transfers between devices with their start and end apart: 10, of which 8 were waited for; matrix products, arithmetic and copies ran while one was open for 12% of the time, Pallas kernels for 0%

commit v1 on v0

--- a/solution.py
+++ b/solution.py
@@ -1,17 +1,511 @@
+import functools
+
 import jax
 import jax.numpy as jnp
 from jax import lax
+from jax.experimental import pallas as pl
+from jax.experimental.pallas import tpu as pltpu
 from jax.sharding import PartitionSpec as P
 
 HEAD_DIM = 64
 NSTATE = 128
 KCONV = 4
+LANES = 128
+PAD = 16
+EPS = 1e-05
+AXES = ("seq", "head", "rep")
+
+f32, bf16 = jnp.float32, jnp.bfloat16
+highest = lax.Precision.HIGHEST
+VMEM_LIMIT = 60 * 1024 * 1024
+
+
+def loop(count, body, carry):
+    if count <= 4:
+        for i in range(count):
+            carry = body(i, carry)
+        return carry
+    return lax.fori_loop(0, count, body, carry)
+
+
+def rows_at(start, size):
+    if isinstance(start, int):
+        return pl.ds(start, size)
+    return pl.ds(pl.multiple_of(start, 8), size)
+
+
+def silu(v):
+    return v / (1.0 + jnp.exp(-v))
+
+
+def place(place_ref, pieces, scratch, blocks, offset=PAD):
+    me = place_ref[0]
+    if len(pieces) == 1:
+        total = pieces[0].shape[0]
+        scratch[pl.ds(offset, total), :] = pieces[0][...].astype(scratch.dtype)
+        return
+    rows = pieces[0].shape[0] // blocks
+    for k, piece in enumerate(pieces):
+        at = me ^ k
+        for block in range(blocks):
+            start = offset + block * rows * len(pieces) + at * rows
+            scratch[rows_at(start, rows), :] = piece[
+                pl.ds(block * rows, rows), :
+            ].astype(scratch.dtype)
+
+
+def aux_kernel(n, blocks, heads, place_ref, *refs):
+    pieces, refs = refs[:n], refs[n:]
+    taps, rates, bt_out, c_out, score_out, rows_out, cum_out, step_out, tail_out, buf = refs
+    total = cum_out.shape[0]
+    span = total // blocks
+    width = 2 * NSTATE
+    buf[pl.ds(0, PAD), :] = jnp.zeros((PAD, buf.shape[1]), f32)
+    place(place_ref, pieces, buf, blocks)
+    first = buf[pl.ds(PAD, total), width + 64 : width + 65] * 256.0
+    first = first + buf[pl.ds(PAD, total), width + 65 : width + 66]
+    position = lax.broadcasted_iota(jnp.int32, (total, 1), 0).astype(f32)
+    live = (position >= first).astype(f32)
+    buf[pl.ds(PAD, total), :width] = jnp.where(live > 0.0, buf[pl.ds(PAD, total), :width], 0.0)
+    lane = lax.broadcasted_iota(jnp.int32, (total, LANES), 1)
+    raw = buf[pl.ds(PAD, total), width : width + LANES] + rates[1:2, :]
+    step = jnp.maximum(raw, 0.0) + jnp.log1p(jnp.exp(-jnp.abs(raw)))
+    step = jnp.where(lane < heads, step * live, 0.0)
+    decay = -rates[0:1, :] * step
+    step_out[...] = jnp.where(lane == LANES - 1, live, step)
+    tail_out[...] = buf[pl.ds(PAD + total - 8, 8), :width].astype(bf16)
+    cum_out[...] = decay
+    q = lax.broadcasted_iota(jnp.int32, (span, span), 0)
+    t = lax.broadcasted_iota(jnp.int32, (span, span), 1)
+    lower = (q >= t).astype(f32)
+
+    def one(block, carry):
+        base = block * span
+        here = rows_at(base, span)
+        cum = jnp.dot(lower, cum_out[here, :], precision=highest, preferred_element_type=f32)
+        cum_out[here, :] = cum
+        lanes = pl.ds(base, span) if isinstance(base, int) else pl.ds(pl.multiple_of(base, LANES), span)
+        cum_t, step_t = cum.T, step_out[here, :].T
+        for pair in range(heads // 2):
+            rows_out[pair, 0:2, lanes] = cum_t[2 * pair : 2 * pair + 2]
+            rows_out[pair, 2:4, lanes] = step_t[2 * pair : 2 * pair + 2]
+        acc = jnp.zeros((span, width), f32)
+        window = buf[rows_at(base + PAD - 8, span + 8), :width]
+        for k in range(KCONV):
+            lo = 8 - KCONV + 1 + k
+            acc = acc + taps[k : k + 1, :] * window[lo : lo + span]
+        conv = silu(acc)
+        b_rows, c_rows = conv[:, :NSTATE], conv[:, NSTATE:].astype(bf16)
+        bt = b_rows.astype(bf16).astype(f32).T.astype(bf16)
+        bt_out[:, lanes] = bt
+        c_out[here, :] = c_rows
+        score_out[here, :] = jnp.dot(c_rows, bt, preferred_element_type=f32) * lower
+        return carry
+
+    loop(blocks, one, 0)
+
+
+def scan_kernel(n, blocks, place_ref, *refs):
+    pieces, refs = refs[:n], refs[n:]
+    params, bt, c_all, scores, row_tables, cum_all, step_all = refs[:7]
+    y_out, state_out, tail_out, buf, cum_e, step_e = refs[7:]
+    total = y_out.shape[0]
+    span = total // blocks
+    pair = pl.program_id(0)
+    buf[pl.ds(0, PAD), :] = jnp.zeros((PAD, LANES), f32)
+    place(place_ref, pieces, buf, blocks)
+    live = step_all[:, LANES - 1 :]
+    buf[pl.ds(PAD, total), :] = jnp.where(live > 0.0, buf[pl.ds(PAD, total), :], 0.0)
+    tail_out[...] = buf[pl.ds(PAD + total - 8, 8), :].astype(bf16)
+    row = lax.broadcasted_iota(jnp.int32, (LANES, LANES), 0)
+    lane = lax.broadcasted_iota(jnp.int32, (LANES, LANES), 1)
+    spread = (row == 2 * pair + lane // HEAD_DIM).astype(f32)
+    cum_e[...] = jnp.dot(cum_all[...], spread, precision=highest, preferred_element_type=f32)
+    step_e[...] = jnp.dot(step_all[...], spread, precision=highest, preferred_element_type=f32)
+    left = lax.broadcasted_iota(jnp.int32, (span, LANES), 1) < HEAD_DIM
+
+    def one(block, state):
+        base = block * span
+        here = rows_at(base, span)
+        lanes = pl.ds(base, span) if isinstance(base, int) else pl.ds(pl.multiple_of(base, LANES), span)
+        acc = jnp.zeros((span, LANES), f32)
+        window = buf[rows_at(base + PAD - 8, span + 8), :]
+        for k in range(KCONV):
+            lo = 8 - KCONV + 1 + k
+            acc = acc + params[k : k + 1, :] * window[lo : lo + span]
+        x_conv = silu(acc).astype(bf16)
+        x_wide = x_conv.astype(f32)
+        cum = cum_e[here, :]
+        last = cum[span - 1 : span, :]
+        score = scores[here, :]
+        parts = []
+        for j in range(2):
+            cum_row = row_tables[0, j : j + 1, lanes]
+            step_row = row_tables[0, 2 + j : 3 + j, lanes]
+            gap = jnp.minimum(cum[:, j * HEAD_DIM : j * HEAD_DIM + 1] - cum_row, 0.0)
+            mix = (score * jnp.exp(gap) * step_row).astype(bf16)
+            parts.append(jnp.dot(mix, x_conv, preferred_element_type=f32))
+        y = jnp.where(left, parts[0], parts[1])
+        c_rows = c_all[here, :]
+        high = state.astype(bf16)
+        low = (state - high.astype(f32)).astype(bf16)
+        entering = jnp.dot(c_rows, high, preferred_element_type=f32)
+        entering = entering + jnp.dot(c_rows, low, preferred_element_type=f32)
+        y_out[here, :] = y + jnp.exp(cum) * entering + params[5:6, :] * x_wide
+        scaled = (jnp.exp(last - cum) * step_e[here, :] * x_wide).astype(bf16)
+        new = jnp.dot(bt[:, lanes], scaled, preferred_element_type=f32)
+        return jnp.exp(last) * state + new
+
+    state = loop(blocks, one, jnp.zeros((NSTATE, LANES), f32))
+    state_out[...] = state.T
+
+
+def project_kernel(n, blocks, seq, tiles, place_ref, *refs):
+    y_ref, refs = refs[0], refs[1:]
+    gates, refs = refs[:n], refs[n:]
+    gain, w_own, w_other, send_out, keep_out, gate_buf, feat, sums = refs
+    step = pl.program_id(0)
+    total = y_ref.shape[0]
+    per = total // seq
+
+    @pl.when(step == 0)
+    def _():
+        place(place_ref, gates, gate_buf, blocks, 0)
+
+        def one(part, carry):
+            here = rows_at(part * per, per)
+            gate = gate_buf[here, :].astype(f32)
+            gated = y_ref[here, :] * silu(gate)
+            square = jnp.sum(gated * gated, axis=1, keepdims=True)
+            sums[part] = jnp.broadcast_to(square, (per, LANES)).T[:8, :]
+            feat[here, :] = (gated * gain[4:5, :]).astype(bf16)
+            return carry
+
+        loop(seq, one, 0)
+
+    def write(out, weight, first):
+        for part in range(seq) if seq <= 4 else ():
+            out[part, :per, :] = jnp.dot(
+                feat[pl.ds(part * per, per), :], weight[...], preferred_element_type=f32
+            ).astype(bf16)
+            out[part, per:, :] = jnp.zeros((8, out.shape[2]), bf16)
+        if seq > 4:
+            @pl.loop(0, seq)
+            def _(part):
+                out[part, :per, :] = jnp.dot(
+                    feat[rows_at(part * per, per), :], weight[...], preferred_element_type=f32
+                ).astype(bf16)
+                out[part, per:, :] = jnp.zeros((8, out.shape[2]), bf16)
+
+        @pl.when(step == first)
+        def _():
+            out[:, per:, :LANES] = sums[...].astype(bf16)
+
+    sending = step < tiles
+    own_now = jnp.where(sending, place_ref[1] == 0, place_ref[1] == 1)
+    for phase, (out, first) in enumerate(((send_out, 0), (keep_out, tiles))):
+        for own, weight in ((True, w_own), (False, w_other)):
+            @pl.when((sending == (phase == 0)) & (own_now == own))
+            def _(out=out, weight=weight, first=first):
+                write(out, weight, first)
+
+
+def finish_kernel(n, inner, *refs):
+    parts, out = refs[:n], refs[n]
+    per = out.shape[0]
+    row = jnp.zeros((1, LANES), f32)
+    for part in parts:
+        row = row + part[per : per + 1, :LANES].astype(f32)
+    scale = lax.rsqrt(row / inner + EPS)
+    scale = jnp.broadcast_to(scale, (LANES, LANES)).T
+    for at in range(0, out.shape[1], LANES):
+        acc = jnp.zeros((per, LANES), f32)
+        for part in parts:
+            acc = acc + part[:per, at : at + LANES].astype(f32)
+        out[:, at : at + LANES] = (acc * scale).astype(bf16)
+
+
+def local(
+    mesh_sizes,
+    x_proj,
+    gate_proj,
+    bc_proj,
+    dt_proj,
+    a_rate,
+    dt_bias,
+    d_skip,
+    conv_x_weight,
+    conv_bc_weight,
+    norm_gain,
+    out_weight,
+    request_first_position,
+    owner,
+):
+    n, n_head, n_rep = mesh_sizes
+    blocks, rows = x_proj.shape[1], x_proj.shape[3]
+    per = blocks * rows
+    total = per * n
+    half_width = x_proj.shape[4]
+    chans = half_width // n
+    heads = chans // HEAD_DIM
+    all_heads = dt_proj.shape[4]
+    inner = half_width * n_head
+    cols = out_weight.shape[1]
+    group = n // n_head
+    fast = rows % 16 == 0
+
+    def dev(s, h, c):
+        return (s * n_head + h) * n_rep + c
+
+    def pairs(rule):
+        return [
+            (dev(s, h, c), dev(*rule(s, h, c)))
+            for s in range(n)
+            for h in range(n_head)
+            for c in range(n_rep)
+        ]
+
+    def move(value, rule):
+        return lax.ppermute(value, AXES, pairs(rule))
+
+    def swap(s, h, c):
+        return (s, c, h)
+
+    seq_at, head_at, rep_at = (lax.axis_index(axis) for axis in AXES)
+    me = (seq_at % group) * n_rep + rep_at
+    half = seq_at // group
+
+    x_in = x_proj.reshape(per, half_width)
+    gate_in = gate_proj.reshape(per, half_width)
+    bc_in = bc_proj.reshape(per, -1)
+    dt_in = dt_proj.reshape(per, all_heads)
+    x_turned = move(x_in, swap)
+
+    start = request_first_position[0]
+    digits = jnp.stack([start // 256, start % 256])
+    facts = jnp.concatenate([digits, owner[0]]).astype(bf16)
+    facts = jnp.broadcast_to(facts[None], (per, n + 2))
+    aux_pad = jnp.zeros((per, 64 - heads), bf16)
+    aux_end = jnp.zeros((per, 64 - n - 2), bf16)
+
+    def aux_for(m):
+        mine = lax.dynamic_slice(dt_in, (0, m * heads), (per, heads))
+        return jnp.concatenate([bc_in, mine, aux_pad, facts, aux_end], axis=1)
+
+    aux = [
+        move(
+            aux_for(seq_at ^ k),
+            lambda s, h, c: (h * group + (s ^ k) // n_rep, c, (s ^ k) % n_rep),
+        )
+        for k in range(n)
+    ]
+    gate_turned = move(gate_in, swap)
+
+    own_chan = me * chans
+    taps = lax.dynamic_slice(conv_x_weight, (0, own_chan), (KCONV, chans))
+    gain = lax.dynamic_slice(norm_gain, (own_chan,), (chans,))[None]
+
+    def per_head(vector):
+        return lax.dynamic_slice(vector, (me * heads,), (heads,))
+
+    vectors = [per_head(v) for v in (d_skip, a_rate, dt_bias)]
+    skip_wide = jnp.repeat(vectors[0], HEAD_DIM)[None]
+    flat = jnp.concatenate(
+        [vectors[1], jnp.zeros((64 - heads,), f32), vectors[2], jnp.zeros((64 - heads,), f32)]
+    )
+    flat = jnp.concatenate([flat, jnp.zeros((chans - 2 * 64,), f32)])[None]
+    packed = jnp.concatenate([taps, gain, skip_wide, flat, jnp.zeros((1, chans), f32)], axis=0)
+    other = lax.ppermute(packed, "head", [(i, (i + 1) % n_head) for i in range(n_head)])
+    params = jnp.where(head_at == half, packed, other)
+    rates = jnp.zeros((8, LANES), f32)
+    rates = rates.at[0, :heads].set(params[6, :heads]).at[1, :heads].set(params[6, 64 : 64 + heads])
+
+    place_info = jnp.stack([me, (head_at == rep_at).astype(jnp.int32)]).astype(jnp.int32)
+
+    def spread(value, width):
+        def rule(k):
+            return lambda s, h, c: (c * group + (s ^ k) // n_rep, h, (s ^ k) % n_rep)
+
+        return [
+            move(lax.dynamic_slice(value, (0, (seq_at ^ k) * width), (per, width)), rule(k))
+            for k in range(n)
+        ]
+
+    def gathered(pieces):
+        if fast:
+            return pieces
+        width = pieces[0].shape[1]
+        full = jnp.zeros((blocks, n, rows, width), pieces[0].dtype)
+        for k, piece in enumerate(pieces):
+            full = lax.dynamic_update_slice(
+                full, piece.reshape(blocks, 1, rows, width), (0, me ^ k, 0, 0)
+            )
+        return [full.reshape(total, width)]
+
+    x_pieces = spread(x_turned, chans)
+    w_other_in, gate_turned = lax.optimization_barrier((out_weight, gate_turned))
+    w_other = lax.ppermute(w_other_in, "head", [(i, (i + 1) % n_head) for i in range(n_head)])
+    gate_pieces = spread(gate_turned, chans)
+
+    def whole(shape):
+        return pl.BlockSpec(shape, lambda *_: (0,) * len(shape))
+
+    def call(kernel, grid, in_specs, out_specs, out_shape, scratch, cost, name):
+        return pl.pallas_call(
+            kernel,
+            grid_spec=pltpu.PrefetchScalarGridSpec(
+                num_scalar_prefetch=1,
+                grid=grid,
+                in_specs=in_specs,
+                out_specs=out_specs,
+                scratch_shapes=scratch,
+            ),
+            out_shape=out_shape,
+            compiler_params=pltpu.CompilerParams(vmem_limit_bytes=VMEM_LIMIT),
+            cost_estimate=pl.CostEstimate(flops=cost, bytes_accessed=4 << 20, transcendentals=0),
+            name=name,
+        )
+
+    shape = jax.ShapeDtypeStruct
+    aux_pieces = gathered(aux)
+    aux_shapes = [
+        ((NSTATE, total), bf16),
+        ((total, NSTATE), bf16),
+        ((total, LANES), f32),
+        ((heads // 2, 8, total), f32),
+        ((total, LANES), f32),
+        ((total, LANES), f32),
+        ((8, 2 * NSTATE), bf16),
+    ]
+    tables = call(
+        functools.partial(aux_kernel, len(aux_pieces), blocks, heads),
+        (1,),
+        [whole(piece.shape) for piece in aux_pieces]
+        + [whole(conv_bc_weight.shape), whole((8, LANES))],
+        [whole(s) for s, _ in aux_shapes],
+        [shape(s, d) for s, d in aux_shapes],
+        [pltpu.VMEM((total + PAD, aux_pieces[0].shape[1]), f32)],
+        3_000_000_000,
+        "aux",
+    )(place_info, *aux_pieces, conv_bc_weight, rates)
+    table_ins, tail_bc = list(tables[:6]), tables[6]
+
+    x_ready = gathered(x_pieces)
+    y, state, tail_x = call(
+        functools.partial(scan_kernel, len(x_ready), blocks),
+        (chans // LANES,),
+        [pl.BlockSpec((piece.shape[0], LANES), lambda i, _: (0, i)) for piece in x_ready]
+        + [pl.BlockSpec((8, LANES), lambda i, _: (0, i))]
+        + [whole(s) for s, _ in aux_shapes[:3]]
+        + [pl.BlockSpec((1, 8, total), lambda i, _: (i, 0, 0))]
+        + [whole(s) for s, _ in aux_shapes[4:6]],
+        [
+            pl.BlockSpec((total, LANES), lambda i, _: (0, i)),
+            pl.BlockSpec((LANES, NSTATE), lambda i, _: (i, 0)),
+            pl.BlockSpec((8, LANES), lambda i, _: (0, i)),
+        ],
+        [shape((total, chans), f32), shape((chans, NSTATE), f32), shape((8, chans), bf16)],
+        [
+            pltpu.VMEM((total + PAD, LANES), f32),
+            pltpu.VMEM((total, LANES), f32),
+            pltpu.VMEM((total, LANES), f32),
+        ],
+        8_000_000_000,
+        "scan",
+    )(place_info, *x_ready, params, *table_ins)
+
+    owner_here = aux[0][0, 2 * NSTATE + 66 : 2 * NSTATE + 66 + n].astype(jnp.int32)
+    slabs = state.astype(bf16).reshape(heads, n, HEAD_DIM // n, NSTATE)
+    rim = KCONV - 1
+    tail_rows = tail_x[8 - rim :].reshape(rim * chans // LANES, LANES)
+    bc_slabs = tail_bc[8 - rim :].reshape(rim, n, -1)
+    bc_wide = bc_slabs.shape[2]
+    slab_rows = heads * (HEAD_DIM // n)
+    tail_count = rim * chans // LANES
+
+    def state_for(target):
+        slab = jnp.sum(jnp.where(owner_here == target, jnp.arange(n, dtype=jnp.int32), 0))
+        mine = lax.dynamic_slice(slabs, (0, slab, 0, 0), (heads, 1, HEAD_DIM // n, NSTATE))
+        mine = mine.reshape(slab_rows, NSTATE)
+        rims = jnp.where(slab == me, tail_rows, jnp.zeros_like(tail_rows))
+        bc_one = lax.dynamic_slice(bc_slabs, (0, slab, 0), (rim, 1, bc_wide)).reshape(rim, bc_wide)
+        bc_one = jnp.pad(bc_one, ((0, 8 - rim), (0, LANES - bc_wide)))
+        return jnp.concatenate([mine, rims, bc_one], axis=0)
+
+    def state_rule(k):
+        return lambda s, h, c: (((s % group) * n_rep + c) ^ k, s // group, h)
+
+    state_parts = [move(state_for(me ^ k), state_rule(k)) for k in range(n)]
+    ssm = jnp.zeros((all_heads, HEAD_DIM // n, NSTATE), f32)
+    rim_x = jnp.zeros((tail_count, LANES), bf16)
+    for k, part in enumerate(state_parts):
+        block = part[:slab_rows].astype(f32).reshape(heads, HEAD_DIM // n, NSTATE)
+        ssm = lax.dynamic_update_slice(ssm, block, ((seq_at ^ k) * heads, 0, 0))
+        rim_x = rim_x + part[slab_rows : slab_rows + tail_count]
+    ssm_state = ssm.reshape(1, 1, all_heads, HEAD_DIM // n * NSTATE)
+    conv_x_state = rim_x.reshape(1, 1, rim, chans)
+    bc_rows = state_parts[0][slab_rows + tail_count :]
+    conv_bc_state = bc_rows[:rim, :bc_wide][None, None]
+
+    gate_ready = gathered(gate_pieces)
+    tile = min(256, cols)
+    tiles = cols // tile
+
+    def weight_at(phase_of_own):
+        def index(j, info):
+            mine = jnp.where(info[1] == 0, 0, 1) if phase_of_own else jnp.where(info[1] == 0, 1, 0)
+            return (0, jnp.clip(j - mine * tiles, 0, tiles - 1))
+
+        return index
+
+    send, keep = call(
+        functools.partial(project_kernel, len(gate_ready), blocks, n, tiles),
+        (2 * tiles,),
+        [whole((total, chans))]
+        + [whole(piece.shape) for piece in gate_ready]
+        + [
+            whole((8, chans)),
+            pl.BlockSpec((chans, tile), weight_at(True)),
+            pl.BlockSpec((chans, tile), weight_at(False)),
+        ],
+        [
+            pl.BlockSpec((n, per + 8, tile), lambda j, _: (0, 0, jnp.minimum(j, tiles - 1))),
+            pl.BlockSpec((n, per + 8, tile), lambda j, _: (0, 0, jnp.maximum(j - tiles, 0))),
+        ],
+        [shape((n, per + 8, cols), bf16)] * 2,
+        [
+            pltpu.VMEM((total, chans), bf16),
+            pltpu.VMEM((total, chans), bf16),
+            pltpu.VMEM((n, 8, LANES), f32),
+        ],
+        4_000_000_000,
+        "project",
+    )(place_info, y, *gate_ready, params, out_weight, w_other)
+
+    came = lax.ppermute(send, "rep", [(i, (i + 1) % n_rep) for i in range(n_rep)])
+
+    def sum_for(target):
+        def pick(value):
+            return lax.dynamic_index_in_dim(value, target, 0, keepdims=False).astype(f32)
+
+        return (pick(keep) + pick(came)).astype(bf16)
+
+    def final_rule(k):
+        return lambda s, h, c: (s ^ k, c, h)
+
+    parts = [move(sum_for(seq_at ^ k), final_rule(k)) for k in range(n)]
+    mixed = pl.pallas_call(
+        functools.partial(finish_kernel, n, float(inner)),
+        out_shape=shape((per, cols), bf16),
+        compiler_params=pltpu.CompilerParams(vmem_limit_bytes=VMEM_LIMIT),
+        name="finish",
+    )(*parts)
+    return (mixed[None], ssm_state, conv_x_state, conv_bc_state)
+
+
 SPAN = 128
 INNER = 8192
-
-
-highest = lax.Precision.HIGHEST
-stability_constant = 1e-05
+stability_constant = EPS
 
 
 def passed_along(value, axis, by):
@@ -91,7 +585,7 @@
     return lax.dynamic_index_in_dim(grouped, slab_index, axis=1, keepdims=False)
 
 
-def local(
+def general(
     x_proj,
     gate_proj,
     bc_proj,
@@ -189,8 +683,11 @@
 
 
 def solution(mesh):
+    sizes = tuple(mesh.shape[axis] for axis in AXES)
+    n, n_head, n_rep = sizes
+    turned = n_head == n_rep == 2 and n & (n - 1) == 0
     return jax.shard_map(
-        local,
+        functools.partial(local, sizes) if turned else general,
         mesh=mesh,
         in_specs=(
             P(("grp", "rep"), None, "seq", None, "head"),

time: 534 us -> 149 us (0.28)
  waiting for transfers between devices: 374 us -> 24 us
  starting transfers between devices: 25.4 us -> 60.8 us
  blocking collectives: 34.7 us -> 0 us
  Pallas kernels: 0 us -> 29.6 us
  local copies, waits for them, and re-layouts: 36.1 us -> 13.2 us
  matrix products: 21.1 us -> 0 us
  other arithmetic: 24.6 us -> 6.69 us
    all_gather x3 -> x0, waiting for transfers between devices: 271 us -> none  [the longest x1 153 us: local(): lax.all_gather(out_weight, ('seq', 'rep'), axis=0, tiled=True)]
    all_to_all x4 -> x0, waiting for transfers between devices: 65.6 us -> none  [the longest x1 48.3 us: local(): lax.all_to_all(gate_proj, 'seq', split_axis=1, concat_axis=2, tiled=True)]
    ppermute x2 -> x25, starting transfers between devices: 5.12 us -> 60.8 us  [the longest x22 44.2 us: move(): return lax.ppermute(value, AXES, pairs(rule))]
    psum x1 -> x0, waiting for transfers between devices: 37.3 us -> none  [local(): final_state = lax.psum(after_decay[:, None, None] * local_final, 'seq')]
    pallas_call x0 -> x4, Pallas kernels: none -> 29.6 us  [the longest x1 13 us: local(): call(functools.partial(scan_kernel, len(x_ready), blocks), (chans // LANE...]
    ppermute x2 -> x25, waiting for transfers between devices: 0.09 us -> 24 us  [the longest x22 24 us: move(): return lax.ppermute(value, AXES, pairs(rule))]
    psum x2 -> x0, blocking collectives: 23.2 us -> none  [the longest x1 18.3 us: broadcast(): return lax.psum(block, axis)]
    dot_general x5 -> x0, matrix products: 21.1 us -> none  [the longest x1 9.45 us: add_rows(): return jnp.dot(source, piece, preferred_element_type=jnp.float32)]
  transfers between devices with their start and end apart: 10 -> 25, of which waited for: 8 -> 5; matrix products, arithmetic and copies ran while one was open for 12% -> 10% of each run, Pallas kernels for 0% -> 19%
where the time goes in v1:
time: 149 us; the launch traced here: 146 us
  starting transfers between devices  60.8 us (41%)
  Pallas kernels  29.6 us (20%)
  waiting for transfers between devices  24 us (16%)
  local copies, waits for them, and re-layouts  13.2 us (9%)
  between operations  12.1 us (8%)
  other arithmetic  6.69 us (4%)
    ppermute x22, starting transfers between devices, move(): return lax.ppermute(value, AXES, pairs(rule))  44.2 us
    ppermute x22, waiting for transfers between devices, move(): return lax.ppermute(value, AXES, pairs(rule))  24 us
    ppermute x1, starting transfers between devices, local(): lax.ppermute(w_other_in, 'head', [(i, (i + 1) % n_head) for i in range(n_...  13.4 us
    pallas_call x1, Pallas kernels, local(): call(functools.partial(scan_kernel, len(x_ready), blocks), (chans // LANE...  13 us
    pallas_call x1, Pallas kernels, local(): call(functools.partial(project_kernel, len(gate_ready), blocks, n, tiles)...  10.7 us
    unnamed x46, local copies, waits for them, and re-layouts  4.11 us
    pallas_call x1, Pallas kernels, local(): call(functools.partial(aux_kernel, len(aux_pieces), blocks, heads), (1,),...  3.78 us
    ppermute x1, starting transfers between devices, local(): lax.ppermute(packed, 'head', [(i, (i + 1) % n_head) for i in range(n_head)])  3.11 us
  transfers between devices with their start and end apart: 25, of which 5 were waited for; matrix products, arithmetic and copies ran while one was open for 10% of the time, Pallas kernels for 19%

profile of v1, /device:TPU:0, one launch (start us, length us, event | category | flops | bytes accessed | tf_op | source)
XLA Modules:
  0.0 146.5 jit_solution(5763273795510156021)
XLA Ops:
  0.7 2.0 %collective-permute-start.10 = (bf16[128,4096]{1,0:T(8,128)(2,1)}, bf16[128,4096]{1,0:T(8,128)(2,1)S(1)}, u32[]{:S(2)}, u32[]{:S(2)}) collective-permute-start(bf16[128,4096]{1,0:T(8,128)(2,1)} %bitcast.90), channel_id=1, source_target_pairs={{0,0},{1,2},{2,1},{3,3},{4,4},{5,6},{6,5},{7,7},{8,8},{9,10},{10,9... | collective-permute-start | bytes 3145736 | tf_op jit(solution)/shard_map/ppermute | solution.py:269
  2.7 0.7 dynamic_slice.107
  3.4 0.7 dynamic_slice.108
  4.1 0.7 dynamic_slice.106
  5.0 0.7 dynamic_slice.105
  5.8 3.1 %collective-permute-start.5 = (f32[8,1024]{1,0:T(8,128)S(1)}, f32[8,1024]{1,0:T(8,128)S(1)}, u32[]{:S(2)}, u32[]{:S(2)}) collective-permute-start(f32[8,1024]{1,0:T(8,128)S(1)} %concatenate.49), channel_id=1, source_target_pairs={{0,2},{2,0},{1,3},{3,1},{4,6},{6,4},{5,7},{7,5},{8,10},{10,8},{9,1... | collective-permute-start | bytes 98312 | tf_op jit(solution)/shard_map/ppermute | solution.py:318
  8.9 1.9 %collective-permute-start = (bf16[128,4096]{1,0:T(8,128)(2,1)}, bf16[128,4096]{1,0:T(8,128)(2,1)S(1)}, u32[]{:S(2)}, u32[]{:S(2)}) collective-permute-start(bf16[128,4096]{1,0:T(8,128)(2,1)} %bitcast.91), channel_id=1, source_target_pairs={{0,0},{1,2},{2,1},{3,3},{4,4},{5,6},{6,5},{7,7},{8,8},{9,10},{10,9... | collective-permute-start | bytes 3145736 | tf_op jit(solution)/shard_map/ppermute | solution.py:269
  11.5 0.7 convert_bitcast_fusion
  12.3 1.0 constant_dynamic-slice_fusion.12
  13.3 1.0 concatenate.54
  14.3 0.7 collective-permute-start.6
  15.0 1.0 concatenate.55
  15.9 3.2 %collective-permute-start.7 = (bf16[128,384]{1,0:T(8,128)(2,1)S(1)}, bf16[128,384]{1,0:T(8,128)(2,1)S(1)}, u32[]{:S(2)}, u32[]{:S(2)}) collective-permute-start(bf16[128,384]{1,0:T(8,128)(2,1)S(1)} %concatenate.55), channel_id=1, source_target_pairs={{0,1},{1,3},{2,9},{3,11},{4,0},{5,2},{6,8},{7,10},{8,5},{9,7},{10,... | collective-permute-start | bytes 294920 | tf_op jit(solution)/shard_map/ppermute | solution.py:269
  19.1 0.6 pad_add_fusion.place_ref
  20.0 0.9 collective-permute-start.8
  20.9 4.8 %collective-permute-start.9 = (bf16[128,384]{1,0:T(8,128)(2,1)S(1)}, bf16[128,384]{1,0:T(8,128)(2,1)S(1)}, u32[]{:S(2)}, u32[]{:S(2)}) collective-permute-start(bf16[128,384]{1,0:T(8,128)(2,1)S(1)} %concatenate.57), channel_id=1, source_target_pairs={{0,5},{1,7},{2,13},{3,15},{4,4},{5,6},{6,12},{7,14},{8,1},{9,3},{1... | collective-permute-start | bytes 294920 | tf_op jit(solution)/shard_map/ppermute | solution.py:269
  26.0 13.4 %collective-permute-start.15 = (bf16[1024,1024]{1,0:T(8,128)(2,1)}, bf16[1024,1024]{1,0:T(8,128)(2,1)}, u32[]{:S(2)}, u32[]{:S(2)}) collective-permute-start(bf16[1024,1024]{1,0:T(8,128)(2,1)} %refs_6_.1), channel_id=1, source_target_pairs={{0,2},{2,0},{1,3},{3,1},{4,6},{6,4},{5,7},{7,5},{8,10},{10,8},{9,1... | collective-permute-start | bytes 6291464 | tf_op jit(solution)/shard_map/ppermute | solution.py:347
  40.1 0.6 copy-done.20
  40.7 3.8 %aux.1 = (bf16[128,512]{1,0:T(8,128)(2,1)}, bf16[512,128]{1,0:T(8,128)(2,1)}, f32[512,128]{1,0:T(8,128)}, f32[8,8,512]{2,1,0:T(8,128)}, f32[512,128]{1,0:T(8,128...) custom-call(s32[2]{0:T(128)} %pad_add_fusion.place_ref, bf16[128,384]{1,0:T(8,128)(2,1)} %copy-done.12, ...), custom_call_target="tpu_custom_call" | custom-call | flops 3000000000 | bytes 4194304 | tf_op jit(solution)/shard_map/aux/pallas_call | solution.py:380
  44.6 5.4 %collective-permute-start.4 = (bf16[128,1024]{1,0:T(8,128)(2,1)S(1)}, bf16[128,1024]{1,0:T(8,128)(2,1)S(1)}, u32[]{:S(2)}, u32[]{:S(2)}) collective-permute-start(bf16[128,1024]{1,0:T(8,128)(2,1)S(1)} %get-tuple-element.68), channel_id=1, source_target_pairs={{0,5},{1,13},{2,7},{3,15},{4,4},{5,12},{6,6},{7,14},{8,1},{9,9},{1... | collective-permute-start | bytes 786440 | tf_op jit(solution)/shard_map/ppermute | solution.py:269
  50.5 1.4 collective-permute-start.1
  51.9 1.5 fusion.15
  63.9 6.2 %collective-permute-start.14 = (bf16[128,1024]{1,0:T(8,128)(2,1)S(1)}, bf16[128,1024]{1,0:T(8,128)(2,1)S(1)}, u32[]{:S(2)}, u32[]{:S(2)}) collective-permute-start(bf16[128,1024]{1,0:T(8,128)(2,1)S(1)} %get-tuple-element.64), channel_id=1, source_target_pairs={{0,5},{1,13},{2,7},{3,15},{4,4},{5,12},{6,6},{7,14},{8,1},{9,9},{1... | collective-permute-start | bytes 786440 | tf_op jit(solution)/shard_map/ppermute | solution.py:269
  70.2 2.1 %collective-permute-start.12 = (bf16[128,1024]{1,0:T(8,128)(2,1)S(1)}, bf16[128,1024]{1,0:T(8,128)(2,1)S(1)}, u32[]{:S(2)}, u32[]{:S(2)}) collective-permute-start(bf16[128,1024]{1,0:T(8,128)(2,1)S(1)} %get-tuple-element.66), channel_id=1, source_target_pairs={{0,1},{1,9},{2,3},{3,11},{4,0},{5,8},{6,2},{7,10},{8,5},{9,13},{10... | collective-permute-start | bytes 786440 | tf_op jit(solution)/shard_map/ppermute | solution.py:269
  72.3 0.7 collective-permute-start.11
  73.0 13.0 %scan.1 = (f32[512,1024]{1,0:T(8,128)}, f32[1024,128]{1,0:T(8,128)}, bf16[8,1024]{1,0:T(8,128)(2,1)}) custom-call(s32[2]{0:T(128)} %pad_add_fusion.place_ref, bf16[128,1024]{1,0:T(8,128)(2,1)} %collective-permute-done.1.refs_0_, bf16[128,1024]{1,0:T(8,128)(2,1)} %collective-permute-done.2.refs_1_, bf16[128,1024]{1,0:T(8,128)(2,1)} %collective-permute-done.3.refs_2_, ...), custom_call_target="tpu_custom_call" | custom-call | flops 8000000000 | bytes 4194304 | tf_op jit(solution)/shard_map/scan/pallas_call | solution.py:394
  86.0 1.1 convert_element_type.94
  87.1 0.7 broadcast_select_fusion.1
  88.0 0.7 collective-permute-start.21
  88.7 2.7 %collective-permute-done.13.refs_3_ = bf16[128,1024]{1,0:T(8,128)(2,1)S(1)} collective-permute-done((bf16[128,1024]{1,0:T(8,128)(2,1)S(1)}, bf16[128,1024]{1,0:T(8,128)(2,1)S(1)}, u32[]{:S(2)}, u32[]{:S(2)}) %collective-permute-start.13) | collective-permute-done | bytes 262176 | tf_op jit(solution)/shard_map/ppermute | solution.py:269
  91.4 5.4 %collective-permute-start.22 = (bf16[288,128]{1,0:T(8,128)(2,1)S(1)}, bf16[288,128]{1,0:T(8,128)(2,1)S(1)}, u32[]{:S(2)}, u32[]{:S(2)}) collective-permute-start(bf16[288,128]{1,0:T(8,128)(2,1)S(1)} %fusion.9), channel_id=1, source_target_pairs={{0,4},{1,0},{2,5},{3,1},{4,12},{5,8},{6,13},{7,9},{8,6},{9,2},{10,... | collective-permute-start | bytes 221192 | tf_op jit(solution)/shard_map/ppermute | solution.py:269
  96.9 0.7 copy-done.16
  97.6 10.7 %project.1 = (bf16[4,136,1024]{2,1,0:T(8,128)(2,1)}, bf16[4,136,1024]{2,1,0:T(8,128)(2,1)}) custom-call(s32[2]{0:T(128)} %pad_add_fusion.place_ref, f32[512,1024]{1,0:T(8,128)} %get-tuple-element.48.refs_0_, bf16[128,1024]{1,0:T(8,128)(2,1)} %copy-done.17, bf16[128,1024]{1,0:T(8,128)(2,1)} %copy-done.16, bf16[128,1024]{1,0:T(8,128)(2,1)} %copy-done.15, ...), custom_call_target="tpu_custom_call" | custom-call | flops 4000000000 | bytes 4194304 | tf_op jit(solution)/shard_map/project/pallas_call | solution.py:461
  108.4 2.9 %collective-permute-start.24 = (bf16[288,128]{1,0:T(8,128)(2,1)S(1)}, bf16[288,128]{1,0:T(8,128)(2,1)S(1)}, u32[]{:S(2)}, u32[]{:S(2)}) collective-permute-start(bf16[288,128]{1,0:T(8,128)(2,1)S(1)} %fusion.11), channel_id=1, source_target_pairs={{0,12},{1,8},{2,13},{3,9},{4,4},{5,0},{6,5},{7,1},{8,14},{9,10},{1... | collective-permute-start | bytes 221192 | tf_op jit(solution)/shard_map/ppermute | solution.py:269
  111.8 2.4 %collective-permute-done.24 = bf16[288,128]{1,0:T(8,128)(2,1)S(1)} collective-permute-done((bf16[288,128]{1,0:T(8,128)(2,1)S(1)}, bf16[288,128]{1,0:T(8,128)(2,1)S(1)}, u32[]{:S(2)}, u32[]{:S(2)}) %collective-permute-start.24) | collective-permute-done | bytes 73760 | tf_op jit(solution)/shard_map/ppermute | solution.py:269
  114.2 2.3 %collective-permute-done.23 = bf16[288,128]{1,0:T(8,128)(2,1)S(1)} collective-permute-done((bf16[288,128]{1,0:T(8,128)(2,1)S(1)}, bf16[288,128]{1,0:T(8,128)(2,1)S(1)}, u32[]{:S(2)}, u32[]{:S(2)}) %collective-permute-start.23) | collective-permute-done | bytes 73760 | tf_op jit(solution)/shard_map/ppermute | solution.py:269
  117.2 1.2 fusion.3
  118.4 3.3 %collective-permute-start.20 = (bf16[136,1024]{1,0:T(8,128)(2,1)}, bf16[136,1024]{1,0:T(8,128)(2,1)S(1)}, u32[]{:S(2)}, u32[]{:S(2)}) collective-permute-start(bf16[136,1024]{1,0:T(8,128)(2,1)} %get-tuple-element.60), channel_id=1, source_target_pairs={{0,12},{1,14},{2,13},{3,15},{4,8},{5,10},{6,9},{7,11},{8,4},{9,6},... | collective-permute-start | bytes 835592 | tf_op jit(solution)/shard_map/ppermute | solution.py:269
  121.8 1.1 collective-permute-start.18
  122.8 0.7 collective-permute-start.17
  123.5 0.7 slice_add_fusion
  124.2 0.9 reshape.223
  125.1 0.6 reshape.224
  126.3 2.9 %collective-permute-done.20.refs_3_ = bf16[136,1024]{1,0:T(8,128)(2,1)S(1)} collective-permute-done((bf16[136,1024]{1,0:T(8,128)(2,1)}, bf16[136,1024]{1,0:T(8,128)(2,1)S(1)}, u32[]{:S(2)}, u32[]{:S(2)}) %collective-permute-start.20) | collective-permute-done | bytes 278560 | tf_op jit(solution)/shard_map/ppermute | solution.py:269
  129.2 13.7 %collective-permute-done.19.refs_2_ = bf16[136,1024]{1,0:T(8,128)(2,1)S(1)} collective-permute-done((bf16[136,1024]{1,0:T(8,128)(2,1)}, bf16[136,1024]{1,0:T(8,128)(2,1)S(1)}, u32[]{:S(2)}, u32[]{:S(2)}) %collective-permute-start.19) | collective-permute-done | bytes 278560 | tf_op jit(solution)/shard_map/ppermute | solution.py:269
  142.8 0.7 copy-done.4
  143.7 0.7 copy-done.6
  144.4 2.1 %finish.1 = bf16[128,1024]{1,0:T(8,128)(2,1)} custom-call(bf16[136,1024]{1,0:T(8,128)(2,1)} %copy-done.6, bf16[136,1024]{1,0:T(8,128)(2,1)} %copy-done.5, bf16[136,1024]{1,0:T(8,128)(2,1)} %copy-done.4, bf16[136,1024]{1,0:T(8,128)(2,1)} %copy-done.3), custom_call_target="tpu_custom_call" | custom-call | tf_op jit(solution)/shard_map/finish/pallas_call | solution.py:497
  (110 shorter events, 4.5 us)
Async XLA Ops:
  0.6 5.2 %copy-start = (f32[4,4096]{1,0:T(4,128)S(1)}, f32[4,4096]{1,0:T(4,128)}, u32[]{:S(2)}) copy-start(f32[4,4096]{1,0:T(4,128)} %param.24) | copy-start | bytes 196612
  0.6 19.1 %copy-start.2 = (bf16[1,4,1,32,256]{4,3,2,1,0:T(8,128)(2,1)S(1)}, bf16[1,4,1,32,256]{4,3,2,1,0:T(8,128)(2,1)}, u32[]{:S(2)}) copy-start(bf16[1,4,1,32,256]{4,3,2,1,0:T(8,128)(2,1)} %param.19) | copy-start | bytes 196612
  0.7 20.3 %collective-permute-start.10 = (bf16[128,4096]{1,0:T(8,128)(2,1)}, bf16[128,4096]{1,0:T(8,128)(2,1)S(1)}, u32[]{:S(2)}, u32[]{:S(2)}) collective-permute-start(bf16[128,4096]{1,0:T(8,128)(2,1)} %bitcast.90), channel_id=1, source_target_pairs={{0,0},{1,2},{2,1},{3,3},{4,4},{5,6},{6,5},{7,7},{8,8},{9,10},{10,9... | collective-permute-start | bytes 3145736 | tf_op jit(solution)/shard_map/ppermute | solution.py:269
  5.8 14.2 %collective-permute-start.5 = (f32[8,1024]{1,0:T(8,128)S(1)}, f32[8,1024]{1,0:T(8,128)S(1)}, u32[]{:S(2)}, u32[]{:S(2)}) collective-permute-start(f32[8,1024]{1,0:T(8,128)S(1)} %concatenate.49), channel_id=1, source_target_pairs={{0,2},{2,0},{1,3},{3,1},{4,6},{6,4},{5,7},{7,5},{8,10},{10,8},{9,1... | collective-permute-start | bytes 98312 | tf_op jit(solution)/shard_map/ppermute | solution.py:318
  8.9 35.6 %collective-permute-start = (bf16[128,4096]{1,0:T(8,128)(2,1)}, bf16[128,4096]{1,0:T(8,128)(2,1)S(1)}, u32[]{:S(2)}, u32[]{:S(2)}) collective-permute-start(bf16[128,4096]{1,0:T(8,128)(2,1)} %bitcast.91), channel_id=1, source_target_pairs={{0,0},{1,2},{2,1},{3,3},{4,4},{5,6},{6,5},{7,7},{8,8},{9,10},{10,9... | collective-permute-start | bytes 3145736 | tf_op jit(solution)/shard_map/ppermute | solution.py:269
  14.3 11.7 %collective-permute-start.6 = (bf16[128,384]{1,0:T(8,128)(2,1)S(1)}, bf16[128,384]{1,0:T(8,128)(2,1)S(1)}, u32[]{:S(2)}, u32[]{:S(2)}) collective-permute-start(bf16[128,384]{1,0:T(8,128)(2,1)S(1)} %concatenate.54), channel_id=1, source_target_pairs={{0,0},{1,2},{2,8},{3,10},{4,1},{5,3},{6,9},{7,11},{8,4},{9,6},{10,... | collective-permute-start | bytes 294920 | tf_op jit(solution)/shard_map/ppermute | solution.py:269
  15.9 23.5 %collective-permute-start.7 = (bf16[128,384]{1,0:T(8,128)(2,1)S(1)}, bf16[128,384]{1,0:T(8,128)(2,1)S(1)}, u32[]{:S(2)}, u32[]{:S(2)}) collective-permute-start(bf16[128,384]{1,0:T(8,128)(2,1)S(1)} %concatenate.55), channel_id=1, source_target_pairs={{0,1},{1,3},{2,9},{3,11},{4,0},{5,2},{6,8},{7,10},{8,5},{9,7},{10,... | collective-permute-start | bytes 294920 | tf_op jit(solution)/shard_map/ppermute | solution.py:269
  20.0 19.4 %collective-permute-start.8 = (bf16[128,384]{1,0:T(8,128)(2,1)S(1)}, bf16[128,384]{1,0:T(8,128)(2,1)S(1)}, u32[]{:S(2)}, u32[]{:S(2)}) collective-permute-start(bf16[128,384]{1,0:T(8,128)(2,1)S(1)} %concatenate.56), channel_id=1, source_target_pairs={{0,4},{1,6},{2,12},{3,14},{4,5},{5,7},{6,13},{7,15},{8,0},{9,2},{1... | collective-permute-start | bytes 294920 | tf_op jit(solution)/shard_map/ppermute | solution.py:269
  20.9 23.6 %copy-start.9 = (f32[8,1024]{1,0:T(8,128)}, f32[8,1024]{1,0:T(8,128)S(1)}, u32[]{:S(2)}) copy-start(f32[8,1024]{1,0:T(8,128)S(1)} %broadcast_select_fusion.refs_4_.refs_5_) | copy-start | bytes 98308
  20.9 18.5 %collective-permute-start.9 = (bf16[128,384]{1,0:T(8,128)(2,1)S(1)}, bf16[128,384]{1,0:T(8,128)(2,1)S(1)}, u32[]{:S(2)}, u32[]{:S(2)}) collective-permute-start(bf16[128,384]{1,0:T(8,128)(2,1)S(1)} %concatenate.57), channel_id=1, source_target_pairs={{0,5},{1,7},{2,13},{3,15},{4,4},{5,6},{6,12},{7,14},{8,1},{9,3},{1... | collective-permute-start | bytes 294920 | tf_op jit(solution)/shard_map/ppermute | solution.py:269
  25.9 13.5 %copy-start.10 = (f32[8,128]{1,0:T(8,128)}, f32[8,128]{1,0:T(8,128)S(1)}, u32[]{:S(2)}) copy-start(f32[8,128]{1,0:T(8,128)S(1)} %scatter.9.refs_5_) | copy-start | bytes 12292
  26.0 13.5 %copy-start.12 = (bf16[128,384]{1,0:T(8,128)(2,1)}, bf16[128,384]{1,0:T(8,128)(2,1)S(1)}, u32[]{:S(2)}) copy-start(bf16[128,384]{1,0:T(8,128)(2,1)S(1)} %collective-permute-done.6.refs_0_) | copy-start | bytes 294916
  26.0 70.8 %collective-permute-start.15 = (bf16[1024,1024]{1,0:T(8,128)(2,1)}, bf16[1024,1024]{1,0:T(8,128)(2,1)}, u32[]{:S(2)}, u32[]{:S(2)}) collective-permute-start(bf16[1024,1024]{1,0:T(8,128)(2,1)} %refs_6_.1), channel_id=1, source_target_pairs={{0,2},{2,0},{1,3},{3,1},{4,6},{6,4},{5,7},{7,5},{8,10},{10,8},{9,1... | collective-permute-start | bytes 6291464 | tf_op jit(solution)/shard_map/ppermute | solution.py:347
  39.4 0.6 copy-start.18
  39.4 0.7 copy-start.19
  40.1 0.7 copy-start.20
  44.5 16.5 %copy-start.11 = (bf16[8,256]{1,0:T(8,128)(2,1)S(1)}, bf16[8,256]{1,0:T(8,128)(2,1)}, u32[]{:S(2)}) copy-start(bf16[8,256]{1,0:T(8,128)(2,1)} %get-tuple-element.55) | copy-start | bytes 12292
  44.6 19.2 %collective-permute-start.4 = (bf16[128,1024]{1,0:T(8,128)(2,1)S(1)}, bf16[128,1024]{1,0:T(8,128)(2,1)S(1)}, u32[]{:S(2)}, u32[]{:S(2)}) collective-permute-start(bf16[128,1024]{1,0:T(8,128)(2,1)S(1)} %get-tuple-element.68), channel_id=1, source_target_pairs={{0,5},{1,13},{2,7},{3,15},{4,4},{5,12},{6,6},{7,14},{8,1},{9,9},{1... | collective-permute-start | bytes 786440 | tf_op jit(solution)/shard_map/ppermute | solution.py:269
  50.0 20.1 %collective-permute-start.3 = (bf16[128,1024]{1,0:T(8,128)(2,1)S(1)}, bf16[128,1024]{1,0:T(8,128)(2,1)}, u32[]{:S(2)}, u32[]{:S(2)}) collective-permute-start(bf16[128,1024]{1,0:T(8,128)(2,1)S(1)} %get-tuple-element.69), channel_id=1, source_target_pairs={{0,4},{1,12},{2,6},{3,14},{4,5},{5,13},{6,7},{7,15},{8,0},{9,8},{1... | collective-permute-start | bytes 786440 | tf_op jit(solution)/shard_map/ppermute | solution.py:269
  50.1 20.1 %collective-permute-start.2 = (bf16[128,1024]{1,0:T(8,128)(2,1)S(1)}, bf16[128,1024]{1,0:T(8,128)(2,1)}, u32[]{:S(2)}, u32[]{:S(2)}) collective-permute-start(bf16[128,1024]{1,0:T(8,128)(2,1)S(1)} %get-tuple-element.70), channel_id=1, source_target_pairs={{0,1},{1,9},{2,3},{3,11},{4,0},{5,8},{6,2},{7,10},{8,5},{9,13},{10... | collective-permute-start | bytes 786440 | tf_op jit(solution)/shard_map/ppermute | solution.py:269
  50.5 21.8 %collective-permute-start.1 = (bf16[128,1024]{1,0:T(8,128)(2,1)S(1)}, bf16[128,1024]{1,0:T(8,128)(2,1)}, u32[]{:S(2)}, u32[]{:S(2)}) collective-permute-start(bf16[128,1024]{1,0:T(8,128)(2,1)S(1)} %get-tuple-element.71), channel_id=1, source_target_pairs={{0,0},{1,8},{2,2},{3,10},{4,1},{5,9},{6,3},{7,11},{8,4},{9,12},{10... | collective-permute-start | bytes 786440 | tf_op jit(solution)/shard_map/ppermute | solution.py:269
  63.9 9.1 %copy-start.13 = (bf16[128,1024]{1,0:T(8,128)(2,1)}, bf16[128,1024]{1,0:T(8,128)(2,1)S(1)}, u32[]{:S(2)}) copy-start(bf16[128,1024]{1,0:T(8,128)(2,1)S(1)} %collective-permute-done.4.refs_3_) | copy-start | bytes 786436
  63.9 24.1 %collective-permute-start.14 = (bf16[128,1024]{1,0:T(8,128)(2,1)S(1)}, bf16[128,1024]{1,0:T(8,128)(2,1)S(1)}, u32[]{:S(2)}, u32[]{:S(2)}) collective-permute-start(bf16[128,1024]{1,0:T(8,128)(2,1)S(1)} %get-tuple-element.64), channel_id=1, source_target_pairs={{0,5},{1,13},{2,7},{3,15},{4,4},{5,12},{6,6},{7,14},{8,1},{9,9},{1... | collective-permute-start | bytes 786440 | tf_op jit(solution)/shard_map/ppermute | solution.py:269
  70.1 21.3 %collective-permute-start.13 = (bf16[128,1024]{1,0:T(8,128)(2,1)S(1)}, bf16[128,1024]{1,0:T(8,128)(2,1)S(1)}, u32[]{:S(2)}, u32[]{:S(2)}) collective-permute-start(bf16[128,1024]{1,0:T(8,128)(2,1)S(1)} %get-tuple-element.65), channel_id=1, source_target_pairs={{0,4},{1,12},{2,6},{3,14},{4,5},{5,13},{6,7},{7,15},{8,0},{9,8},{1... | collective-permute-start | bytes 786440 | tf_op jit(solution)/shard_map/ppermute | solution.py:269
  70.2 26.6 %collective-permute-start.12 = (bf16[128,1024]{1,0:T(8,128)(2,1)S(1)}, bf16[128,1024]{1,0:T(8,128)(2,1)S(1)}, u32[]{:S(2)}, u32[]{:S(2)}) collective-permute-start(bf16[128,1024]{1,0:T(8,128)(2,1)S(1)} %get-tuple-element.66), channel_id=1, source_target_pairs={{0,1},{1,9},{2,3},{3,11},{4,0},{5,8},{6,2},{7,10},{8,5},{9,13},{10... | collective-permute-start | bytes 786440 | tf_op jit(solution)/shard_map/ppermute | solution.py:269
  72.3 24.5 %collective-permute-start.11 = (bf16[128,1024]{1,0:T(8,128)(2,1)S(1)}, bf16[128,1024]{1,0:T(8,128)(2,1)S(1)}, u32[]{:S(2)}, u32[]{:S(2)}) collective-permute-start(bf16[128,1024]{1,0:T(8,128)(2,1)S(1)} %get-tuple-element.67), channel_id=1, source_target_pairs={{0,0},{1,8},{2,2},{3,10},{4,1},{5,9},{6,3},{7,11},{8,4},{9,12},{10... | collective-permute-start | bytes 786440 | tf_op jit(solution)/shard_map/ppermute | solution.py:269
  88.0 8.8 %copy-start.14 = (bf16[128,1024]{1,0:T(8,128)(2,1)}, bf16[128,1024]{1,0:T(8,128)(2,1)S(1)}, u32[]{:S(2)}) copy-start(bf16[128,1024]{1,0:T(8,128)(2,1)S(1)} %collective-permute-done.14.refs_4_) | copy-start | bytes 786436
  88.0 23.7 %collective-permute-start.21 = (bf16[288,128]{1,0:T(8,128)(2,1)S(1)}, bf16[288,128]{1,0:T(8,128)(2,1)S(1)}, u32[]{:S(2)}, u32[]{:S(2)}) collective-permute-start(bf16[288,128]{1,0:T(8,128)(2,1)S(1)} %fusion.8), channel_id=1, source_target_pairs={{0,0},{1,4},{2,1},{3,5},{4,8},{5,12},{6,9},{7,13},{8,2},{9,6},{10,... | collective-permute-start | bytes 221192 | tf_op jit(solution)/shard_map/ppermute | solution.py:269
  91.4 5.4 %copy-start.15 = (bf16[128,1024]{1,0:T(8,128)(2,1)}, bf16[128,1024]{1,0:T(8,128)(2,1)S(1)}, u32[]{:S(2)}) copy-start(bf16[128,1024]{1,0:T(8,128)(2,1)S(1)} %collective-permute-done.13.refs_3_) | copy-start | bytes 786436
  91.4 20.4 %collective-permute-start.22 = (bf16[288,128]{1,0:T(8,128)(2,1)S(1)}, bf16[288,128]{1,0:T(8,128)(2,1)S(1)}, u32[]{:S(2)}, u32[]{:S(2)}) collective-permute-start(bf16[288,128]{1,0:T(8,128)(2,1)S(1)} %fusion.9), channel_id=1, source_target_pairs={{0,4},{1,0},{2,5},{3,1},{4,12},{5,8},{6,13},{7,9},{8,6},{9,2},{10,... | collective-permute-start | bytes 221192 | tf_op jit(solution)/shard_map/ppermute | solution.py:269
  96.8 0.7 copy-start.16
  96.8 0.8 copy-start.17
  108.3 8.9 %copy-start.1 = (bf16[4,136,1024]{2,1,0:T(8,128)(2,1)S(1)}, bf16[4,136,1024]{2,1,0:T(8,128)(2,1)}, u32[]{:S(2)}) copy-start(bf16[4,136,1024]{2,1,0:T(8,128)(2,1)} %get-tuple-element.51) | copy-start | bytes 3342340
  108.3 8.4 %collective-permute-start.16 = (bf16[4,136,1024]{2,1,0:T(8,128)(2,1)}, bf16[4,136,1024]{2,1,0:T(8,128)(2,1)S(1)}, u32[]{:S(2)}, u32[]{:S(2)}) collective-permute-start(bf16[4,136,1024]{2,1,0:T(8,128)(2,1)} %get-tuple-element.52), channel_id=1, source_target_pairs={{0,1},{1,0},{2,3},{3,2},{4,5},{5,4},{6,7},{7,6},{8,9},{9,8},{10,11... | collective-permute-start | bytes 3342344 | tf_op jit(solution)/shard_map/ppermute | solution.py:485
  108.4 5.8 %collective-permute-start.24 = (bf16[288,128]{1,0:T(8,128)(2,1)S(1)}, bf16[288,128]{1,0:T(8,128)(2,1)S(1)}, u32[]{:S(2)}, u32[]{:S(2)}) collective-permute-start(bf16[288,128]{1,0:T(8,128)(2,1)S(1)} %fusion.11), channel_id=1, source_target_pairs={{0,12},{1,8},{2,13},{3,9},{4,4},{5,0},{6,5},{7,1},{8,14},{9,10},{1... | collective-permute-start | bytes 221192 | tf_op jit(solution)/shard_map/ppermute | solution.py:269
  111.3 5.2 %collective-permute-start.23 = (bf16[288,128]{1,0:T(8,128)(2,1)S(1)}, bf16[288,128]{1,0:T(8,128)(2,1)S(1)}, u32[]{:S(2)}, u32[]{:S(2)}) collective-permute-start(bf16[288,128]{1,0:T(8,128)(2,1)S(1)} %fusion.10), channel_id=1, source_target_pairs={{0,8},{1,12},{2,9},{3,13},{4,0},{5,4},{6,1},{7,5},{8,10},{9,14},{1... | collective-permute-start | bytes 221192 | tf_op jit(solution)/shard_map/ppermute | solution.py:269
  114.2 2.4 %copy-start.7 = (bf16[288,128]{1,0:T(8,128)(2,1)}, bf16[288,128]{1,0:T(8,128)(2,1)S(1)}, u32[]{:S(2)}) copy-start(bf16[288,128]{1,0:T(8,128)(2,1)S(1)} %collective-permute-done.24) | copy-start | bytes 221188
  116.6 0.6 copy-start.8
  118.4 10.7 %collective-permute-start.20 = (bf16[136,1024]{1,0:T(8,128)(2,1)}, bf16[136,1024]{1,0:T(8,128)(2,1)S(1)}, u32[]{:S(2)}, u32[]{:S(2)}) collective-permute-start(bf16[136,1024]{1,0:T(8,128)(2,1)} %get-tuple-element.60), channel_id=1, source_target_pairs={{0,12},{1,14},{2,13},{3,15},{4,8},{5,10},{6,9},{7,11},{8,4},{9,6},... | collective-permute-start | bytes 835592 | tf_op jit(solution)/shard_map/ppermute | solution.py:269
  121.7 21.1 %collective-permute-start.19 = (bf16[136,1024]{1,0:T(8,128)(2,1)}, bf16[136,1024]{1,0:T(8,128)(2,1)S(1)}, u32[]{:S(2)}, u32[]{:S(2)}) collective-permute-start(bf16[136,1024]{1,0:T(8,128)(2,1)} %get-tuple-element.61), channel_id=1, source_target_pairs={{0,8},{1,10},{2,9},{3,11},{4,12},{5,14},{6,13},{7,15},{8,0},{9,2},... | collective-permute-start | bytes 835592 | tf_op jit(solution)/shard_map/ppermute | solution.py:269
  121.8 21.1 %collective-permute-start.18 = (bf16[136,1024]{1,0:T(8,128)(2,1)S(1)}, bf16[136,1024]{1,0:T(8,128)(2,1)S(1)}, u32[]{:S(2)}, u32[]{:S(2)}) collective-permute-start(bf16[136,1024]{1,0:T(8,128)(2,1)S(1)} %get-tuple-element.62), channel_id=1, source_target_pairs={{0,4},{1,6},{2,5},{3,7},{4,0},{5,2},{6,1},{7,3},{8,12},{9,14},{10,... | collective-permute-start | bytes 835592 | tf_op jit(solution)/shard_map/ppermute | solution.py:269
  122.8 20.0 %collective-permute-start.17 = (bf16[136,1024]{1,0:T(8,128)(2,1)S(1)}, bf16[136,1024]{1,0:T(8,128)(2,1)S(1)}, u32[]{:S(2)}, u32[]{:S(2)}) collective-permute-start(bf16[136,1024]{1,0:T(8,128)(2,1)S(1)} %get-tuple-element.63), channel_id=1, source_target_pairs={{0,0},{1,2},{2,1},{3,3},{4,4},{5,6},{6,5},{7,7},{8,8},{9,10},{10,9... | collective-permute-start | bytes 835592 | tf_op jit(solution)/shard_map/ppermute | solution.py:269
  129.2 13.7 %copy-start.3 = (bf16[136,1024]{1,0:T(8,128)(2,1)}, bf16[136,1024]{1,0:T(8,128)(2,1)S(1)}, u32[]{:S(2)}) copy-start(bf16[136,1024]{1,0:T(8,128)(2,1)S(1)} %collective-permute-done.20.refs_3_) | copy-start | bytes 835588
  142.8 0.7 copy-start.4
  142.8 0.8 copy-start.5
  143.7 0.7 copy-start.6
